TPU v7x, 32 devices: a whole 2x2x4 slice. The times are simulated.
32 devices in a mesh: band: 8 (over z, x), grid: 4 (over y, core).
Axes of the slice: x: 2, y: 2, z: 4, core: 2. Of those that a mesh axis runs over, the one named last changes fastest.
Arguments:
- partial_density: float32 [8, 128, 128, 128], P('band', 'grid'), may hold values from 0.01 to 1
- node_index: int32 [128, 128, 128], P('grid'), may hold values from 0 to 19
- node_weight: float32 [4, 128, 128, 128], P(None, 'grid'), may hold values from 0 to 1
- node_slope: float32 [4, 128, 128, 128], P(None, 'grid'), may hold values from -6 to 6
- kernel_table: float32 [20, 20, 114], replicated, may hold values from -0.8 to 0.8, as said below
Outputs:
- potential: float32 [128, 128, 128], P('grid')
Inputs may be any that keep to these rules, and one draw needn't show every extreme that they name: node_index(r) is the node at the lower end of the interval of q0 at r; nodes node_index - 1 to node_index + 2 carry the four weights. `kernel_table`: symmetric in its first two indices.
All inputs are finite; a program needn't handle non-finite values.
Results may differ from a plain program's by a relative error of at most 0.0003.
Values sent between devices are 32-bit elements; how exact they have to be, the bound alone decides.
A program may use at most 128 MiB of HBM per device.

v0:
```python
import math
import jax
import jax.numpy as jnp
from jax import lax
from jax.sharding import PartitionSpec as P

N = 128


def frequency_of(positions, length):
    return jnp.where(positions < length // 2, positions, positions - length)


def shell_split(square_norm):
    root_value = jnp.sqrt(square_norm.astype(jnp.float32))
    shell_idx = root_value.astype(jnp.int32)
    shell_idx = shell_idx - (shell_idx * shell_idx > square_norm).astype(jnp.int32)
    shell_idx = shell_idx + ((shell_idx + 1) * (shell_idx + 1) <= square_norm).astype(jnp.int32)
    fraction = root_value - shell_idx.astype(jnp.float32)
    return (shell_idx, fraction)


def node_fields(count_nodes, intervals, weights):
    node_ids = jnp.arange(count_nodes, dtype=jnp.int32)
    summed = jnp.zeros((count_nodes,) + intervals.shape, jnp.float32)
    for offset in range(4):
        matched = node_ids[:, None, None, None] == (intervals + (offset - 1))[None]
        summed = summed + jnp.where(matched, weights[offset][None], jnp.zeros((), jnp.float32))
    return summed


def phase_table(source_idx, target_idx, modulus):
    product_mod = source_idx[:, None] * target_idx[None, :] % modulus
    angles = product_mod.astype(jnp.float32) * (2.0 * math.pi / modulus)
    return (jnp.cos(angles), jnp.sin(angles))


def contract(pattern, operand, matrix):
    return jnp.einsum(pattern, operand, matrix, precision=lax.Precision.HIGHEST)


def mirrored(values, dim):
    return jnp.roll(jnp.flip(values, dim), 1, dim)


def forward_tables(positions, plane_ids, length):
    cosine, sine = phase_table(positions, plane_ids, length)
    alternating = jnp.where(positions % 2 == 0, 1.0, -1.0).astype(jnp.float32)
    sine = jnp.where(plane_ids[None, :] == 0, -alternating[:, None], sine)
    return (cosine, sine)


def shell_weights_of(square_norm, shell_count):
    shell_ids = jnp.arange(shell_count, dtype=jnp.int32)
    shell_idx, fraction = shell_split(square_norm)
    expand = (slice(None),) + (None,) * square_norm.ndim
    lower_hit = shell_ids[expand] == shell_idx[None]
    upper_hit = shell_ids[expand] == shell_idx[None] + 1
    return jnp.where(lower_hit, 1.0 - fraction[None], 0.0) + jnp.where(
        upper_hit, fraction[None], 0.0
    )


def per_device(partial_density, node_index, node_weight, node_slope, kernel_table):
    length = N
    half = length // 2
    count_nodes = kernel_table.shape[0]
    shell_count = kernel_table.shape[2]
    planes = half // lax.axis_size("band")
    grid_part = length // lax.axis_size("grid")
    band_at = lax.axis_index("band")
    grid_at = lax.axis_index("grid")
    full_range = jnp.arange(length, dtype=jnp.int32)
    own_planes = band_at * planes + jnp.arange(planes, dtype=jnp.int32)
    own_rows = grid_at * grid_part + jnp.arange(grid_part, dtype=jnp.int32)
    first_band = band_at == 0
    lower_rows = (full_range >= 1) & (full_range < half)
    upper_rows = full_range > half
    density = lax.psum(partial_density[0], "band")
    theta_fields = density[None] * node_fields(count_nodes, node_index, node_weight)
    cosine_z, sine_z = forward_tables(full_range, own_planes, length)
    forward_real = contract("axyz,zk->axyk", theta_fields, cosine_z)
    forward_imag = -contract("axyz,zk->axyk", theta_fields, sine_z)
    columns = jnp.stack([forward_real, forward_imag])
    cosine_full, sine_full = phase_table(full_range, full_range, length)
    y_cos = contract("caxyp,yw->caxpw", columns, cosine_full)
    y_sin = contract("caxyp,yw->caxpw", columns, sine_full)
    ywave_real = y_cos[0] + y_sin[1]
    ywave_imag = y_cos[1] - y_sin[0]
    first_real = ywave_real[:, :, 0, :]
    first_imag = ywave_imag[:, :, 0, :]
    turned_real = mirrored(first_real, 2)
    turned_imag = mirrored(first_imag, 2)
    packed_real = jnp.where(
        lower_rows,
        0.5 * (first_real + turned_real),
        jnp.where(upper_rows, 0.5 * (turned_imag + first_imag), first_real),
    )
    packed_imag = jnp.where(
        lower_rows,
        0.5 * (first_imag - turned_imag),
        jnp.where(upper_rows, 0.5 * (first_real - turned_real), first_imag),
    )
    ywave_real = ywave_real.at[:, :, 0, :].set(jnp.where(first_band, packed_real, first_real))
    ywave_imag = ywave_imag.at[:, :, 0, :].set(jnp.where(first_band, packed_imag, first_imag))
    pencils = lax.all_to_all(
        jnp.stack([ywave_real, ywave_imag]), "grid", split_axis=4, concat_axis=2, tiled=True
    )
    x_cos = contract("caxpw,xv->capwv", pencils, cosine_full)
    x_sin = contract("caxpw,xv->capwv", pencils, sine_full)
    spec_real = x_cos[0] + x_sin[1]
    spec_imag = x_cos[1] - x_sin[0]
    freq_x = frequency_of(full_range, length)
    square_x = freq_x * freq_x
    freq_rows = frequency_of(own_rows, length)
    plane_square = own_planes * own_planes
    third_square = jnp.where(
        (own_planes[:, None] == 0) & (own_rows[None, :] > half), half * half, plane_square[:, None]
    )
    special_rows = ((own_rows == 0) | (own_rows == half)) & (own_planes[0] == 0)

    def mix_row(row_idx):
        row_real = lax.dynamic_index_in_dim(spec_real, row_idx, 2, keepdims=False)
        row_imag = lax.dynamic_index_in_dim(spec_imag, row_idx, 2, keepdims=False)
        freq_row = lax.dynamic_index_in_dim(freq_rows, row_idx, 0, keepdims=False)
        third_row = lax.dynamic_index_in_dim(third_square, row_idx, 1, keepdims=False)
        square_norm = third_row[:, None] + square_x[None, :] + freq_row * freq_row
        kernel = contract("abs,spx->abpx", kernel_table, shell_weights_of(square_norm, shell_count))
        out_real = contract("abpx,apx->bpx", kernel, row_real)
        out_imag = contract("abpx,apx->bpx", kernel, row_imag)
        other_norm = square_x + freq_row * freq_row + half * half
        kernel_other = contract(
            "abs,sx->abx", kernel_table, shell_weights_of(other_norm, shell_count)
        )
        flag = lax.dynamic_index_in_dim(special_rows, row_idx, 0, keepdims=False).astype(
            jnp.float32
        )
        spread = 0.5 * flag * (kernel[:, :, 0, :] - kernel_other)
        base_real = row_real[:, 0, :]
        base_imag = row_imag[:, 0, :]
        delta_real = mirrored(base_real, 1) - base_real
        delta_imag = -mirrored(base_imag, 1) - base_imag
        out_real = out_real.at[:, 0, :].add(contract("abx,ax->bx", spread, delta_real))
        out_imag = out_imag.at[:, 0, :].add(contract("abx,ax->bx", spread, delta_imag))
        return jnp.stack([out_real, out_imag])

    mixed = lax.map(mix_row, jnp.arange(grid_part, dtype=jnp.int32))
    i_cos = contract("wcbpx,xv->wcbpv", mixed, cosine_full)
    i_sin = contract("wcbpx,xv->wcbpv", mixed, sine_full)
    inverse_real = i_cos[:, 0] - i_sin[:, 1]
    inverse_imag = i_cos[:, 1] + i_sin[:, 0]
    returned = lax.all_to_all(
        jnp.stack([inverse_real, inverse_imag], axis=1),
        "grid",
        split_axis=4,
        concat_axis=0,
        tiled=True,
    )
    lower_col = lower_rows[:, None, None]
    upper_col = upper_rows[:, None, None]
    back_real = returned[:, 0, :, 0, :]
    back_imag = returned[:, 1, :, 0, :]
    flip_real = mirrored(back_real, 0)
    flip_imag = mirrored(back_imag, 0)
    joined_real = jnp.where(
        lower_col, back_real - flip_imag, jnp.where(upper_col, flip_real + back_imag, back_real)
    )
    joined_imag = jnp.where(
        lower_col, back_imag + flip_real, jnp.where(upper_col, back_real - flip_imag, back_imag)
    )
    returned = returned.at[:, 0, :, 0, :].set(jnp.where(first_band, joined_real, back_real))
    returned = returned.at[:, 1, :, 0, :].set(jnp.where(first_band, joined_imag, back_imag))
    b_cos = contract("wcbpx,wy->cbpxy", returned, cosine_full)
    b_sin = contract("wcbpx,wy->cbpxy", returned, sine_full)
    slab_real = b_cos[0] - b_sin[1]
    slab_imag = b_cos[1] + b_sin[0]
    cosine_own, sine_own = phase_table(own_planes, full_range, length)
    alternating = jnp.where(full_range % 2 == 0, 1.0, -1.0).astype(jnp.float32)
    cosine_back = jnp.where(own_planes[:, None] == 0, 1.0, 2.0 * cosine_own)
    sine_back = jnp.where(own_planes[:, None] == 0, -alternating[None, :], 2.0 * sine_own)
    scale_factor = 1.0 / float(length) ** 3
    field_parts = (
        contract("bpxy,pz->bxyz", slab_real, cosine_back)
        - contract("bpxy,pz->bxyz", slab_imag, sine_back)
    ) * scale_factor
    slopes = node_fields(count_nodes, node_index, node_slope)
    partial_potential = jnp.sum(field_parts * slopes, axis=0)
    return lax.psum(partial_potential, "band")


def solution(mesh):
    placed = (
        P("band", "grid", None, None),
        P("grid", None, None),
        P(None, "grid", None, None),
        P(None, "grid", None, None),
        P(),
    )
    return jax.shard_map(
        per_device, mesh=mesh, in_specs=placed, out_specs=P("grid", None, None), check_vma=False
    )
```

profile of v0, /device:TPU:0, one launch (start us, length us, event | category | flops | bytes accessed | tf_op | source)
XLA Modules:
  0.0 1415.7 jit_solution(10311914120012794032)
XLA Ops:
  17.1 98.9 %all-reduce.3.cloned.1.call-done = f32[32,128,128]{2,1,0:T(8,128)} async-done(((f32[32,128,128]{2,1,0:T(8,128)}), f32[32,128,128]{2,1,0:T(8,128)}) %all-reduce.3.cloned.1.call-update) | async-done | bytes 2097168 | tf_op jit(solution)/shard_map/psum | solution.py:79
  116.0 66.0 %fusion.70 = f32[1,20,32,128,8]{3,4,2,1,0:T(8,128)} fusion(f32[32,128,128]{2,1,0:T(8,128)} %get-tuple-element.295, s32[32,128,128]{2,1,0:T(8,128)} %get-tuple-element.309, f32[32,128,128]{2,1,0:T(8,128)} %get-tuple-element.296, s32[32,128,128]{2,1,0:T(8,128)} %get-tuple-element.310, f32[32,128,128]{2,1,0:T(8,128)} %get-tuple-element.294, ...), kind=kOutput, calls=%fused_computation.132 | convolution fusion | flops 1132476416 | bytes 21495840 | tf_op jit(solution)/shard_map/axyz,zk->axyk/dot_general | solution.py:39
  182.0 57.5 %negate_bitcast_fusion = f32[1,20,32,128,8]{3,4,2,1,0:T(8,128)} fusion(f32[32,128,128]{2,1,0:T(8,128)} %get-tuple-element.295, s32[32,128,128]{2,1,0:T(8,128)} %get-tuple-element.309, f32[32,128,128]{2,1,0:T(8,128)} %get-tuple-element.296, s32[32,128,128]{2,1,0:T(8,128)} %get-tuple-element.310, f32[32,128,128]{2,1,0:T(8,128)} %get-tuple-element.294, ...), kind=kOutput, calls=%fused_computation.123 | convolution fusion | flops 1133132800 | bytes 21496360 | tf_op jit(solution)/shard_map/axyz,zk->axyk/dot_general | solution.py:39
  266.0 7.4 scatter.15
  273.4 9.3 scatter.14
  287.3 17.6 %copy.61 = f32[2,20,32,8,128]{2,3,1,0,4:T(8,128)} copy(f32[2,20,32,8,128]{4,3,2,1,0:T(8,128)} %pad_maximum_fusion.1) | data formatting | bytes 10485760 | tf_op jit(solution)/shard_map/stack | solution.py:107
  304.9 23.5 %reshape.667 = f32[4,1,327680]{2,1,0:T(1,128)} reshape(f32[128,2,20,8,32]{4,3,2,1,0:T(8,128)} %bitcast.306) | data formatting | bytes 10485760
  333.6 59.3 %all-to-all-done = f32[4,1,327680]{2,1,0:T(1,128)} async-done(((f32[4,1,327680]{2,1,0:T(1,128)}), f32[4,1,327680]{2,1,0:T(1,128)}, u32[]{:S(2)}, u32[]{:S(2)}) %all-to-all-start) | async-done | bytes 5242912 | tf_op jit(solution)/shard_map/all_to_all | solution.py:106
  393.5 17.9 %reduce.21 = f32[4,327680]{1,0:T(4,128)} reduce(f32[4,1,327680]{2,1,0:T(1,128)} %all-to-all-done, f32[]{:T(128)} %broadcast.766), dimensions={1}, to_apply=%all_to_all.26.reduce_sub_computation | reduce | bytes 10485764 | tf_op jit(solution)/shard_map/all_to_all | solution.py:106
  411.4 16.7 %reshape.668 = f32[128,2,20,8,32]{4,3,2,1,0:T(8,128)} reshape(f32[4,327680]{1,0:T(4,128)} %reduce.21) | data formatting | bytes 10485760
  428.1 25.8 %copy.142 = f32[2,20,32,8,4,32]{2,4,5,3,1,0:T(4,128)} copy(f32[2,20,32,8,4,32]{2,3,1,0,5,4:T(8,128)} %bitcast.307) | data formatting | bytes 10485760 | tf_op jit(solution)/shard_map/all_to_all | solution.py:106
  453.9 16.5 %all_to_all.29 = f32[2,20,128,8,32]{2,4,3,1,0:T(8,128)} reshape(f32[2,20,4,32,8,32]{3,2,5,4,1,0:T(4,128)} %bitcast.308) | data formatting | bytes 10485760 | tf_op jit(solution)/shard_map/all_to_all | solution.py:106
  470.4 8.7 fusion.81
  486.7 425.2 %while.20 = (s32[]{:T(128)}, f32[32,2,20,8,128]{4,3,2,1,0:T(8,128)}, s32[32]{0:T(128)S(1)}, f32[20,8,32,128]{3,2,1,0:T(8,128)}, s32[8,32]{0,1:T(8,128)S(1)}, /*i...) while((s32[]{:T(128)}, ...), condition=%wide.region_2.3_spmd.clone.clone, body=%wide.region_1.2_spmd.clone.clone.sunk | while | flops 633025536 | bytes 4581378 | solution.py:147
  927.4 17.5 %copy.63 = f32[32,2,20,8,128]{0,3,2,1,4:T(8,128)} copy(f32[32,2,20,8,128]{4,3,2,1,0:T(8,128)} %pad_maximum_fusion.2) | data formatting | bytes 10485760 | tf_op jit(solution)/shard_map/stack | solution.py:153
  945.0 23.5 %reshape.669 = f32[4,1,327680]{2,1,0:T(1,128)} reshape(f32[128,2,20,8,32]{4,3,2,1,0:T(8,128)} %bitcast.309) | data formatting | bytes 10485760
  979.9 53.0 %all-to-all-done.1 = f32[4,1,327680]{2,1,0:T(1,128)} async-done(((f32[4,1,327680]{2,1,0:T(1,128)}), f32[4,1,327680]{2,1,0:T(1,128)}, u32[]{:S(2)}, u32[]{:S(2)}) %all-to-all-start.1) | async-done | bytes 5242912 | tf_op jit(solution)/shard_map/all_to_all | solution.py:152
  1033.0 18.3 %reduce.22 = f32[4,327680]{1,0:T(4,128)} reduce(f32[4,1,327680]{2,1,0:T(1,128)} %all-to-all-done.1, f32[]{:T(128)} %broadcast.766), dimensions={1}, to_apply=%all_to_all.30.reduce_sub_computation | reduce | bytes 10485764 | tf_op jit(solution)/shard_map/all_to_all | solution.py:152
  1051.3 16.7 %reshape.670 = f32[128,2,20,8,32]{4,3,2,1,0:T(8,128)} reshape(f32[4,327680]{1,0:T(4,128)} %reduce.22) | data formatting | bytes 10485760
  1068.0 25.5 %copy.64 = f32[4,32,2,20,8,32]{1,0,5,3,4,2:T(4,128)} copy(f32[4,32,2,20,8,32]{1,4,3,2,5,0:T(8,128)} %bitcast.310) | data formatting | bytes 10485760 | tf_op jit(solution)/shard_map/all_to_all | solution.py:152
  1093.5 16.6 %all_to_all.33 = f32[128,2,20,8,32]{0,4,2,3,1:T(8,128)} reshape(f32[4,32,2,20,8,32]{1,0,5,3,4,2:T(4,128)} %copy.64) | data formatting | bytes 10485760 | tf_op jit(solution)/shard_map/all_to_all | solution.py:152
  1138.9 69.8 %fusion.68 = f32[20,32,128,128]{3,2,1,0:T(8,128)} fusion(f32[20,8,32,128]{3,2,1,0:T(8,128)S(1)} %get-tuple-element.284, s32[8]{0:T(128)S(1)} %iota_add_fusion.1, pred[8]{0:T(512)(128)(4,1)S(1)} %broadcast_compare_fusion), kind=kOutput, calls=%fused_computation.121 | convolution fusion | flops 1006649344 | bytes 44564520 | tf_op jit(solution)/shard_map/bpxy,pz->bxyz/dot_general | solution.py:39
  1208.8 95.9 %multiply_reduce_fusion.4 = f32[32,128,128]{2,1,0:T(8,128)} fusion(f32[20,32,128,128]{3,2,1,0:T(8,128)} %fusion.68, f32[32,128,128]{2,1,0:T(8,128)S(1)} %copy-done.6, f32[32,128,128]{2,1,0:T(8,128)S(1)} %copy-done.7, f32[32,128,128]{2,1,0:T(8,128)S(1)} %copy-done.5, f32[32,128,128]{2,1,0:T(8,128)S(1)} %get-tuple-element.289, ...), kind=kOutput, calls=%fused_computation.74 | convolution fusion | flops 1163411456 | bytes 63439400 | tf_op jit(solution)/shard_map/bpxy,pz->bxyz/dot_general | solution.py:39
  1304.7 100.9 %all-reduce.5.cloned.1.call-done = f32[32,128,128]{2,1,0:T(8,128)} async-done(((f32[32,128,128]{2,1,0:T(8,128)}), f32[32,128,128]{2,1,0:T(8,128)}) %all-reduce.5.cloned.1.call-update) | async-done | bytes 2097168 | tf_op jit(solution)/shard_map/psum | solution.py:188
  (1141 shorter events, 410.1 us)
Async XLA Ops:
  6.5 109.5 %all-reduce.3.cloned.1.call-start = ((), (), s32[]{:S(2)}) async-start(), calls=%async_computation.2 | async-start | bytes 4194304 | tf_op jit(solution)/shard_map/psum | solution.py:79
  7.3 6.2 copy-start.12
  7.3 174.7 %copy-start.14 = (f32[128]{0:T(128)}, f32[128]{0:T(128)S(1)}, u32[]{:S(2)}) copy-start(f32[128]{0:T(128)S(1)} %fusion.141) | copy-start | bytes 1540
  13.5 102.5 %copy-start = (s32[32,128,128]{2,1,0:T(8,128)S(1)}, s32[32,128,128]{2,1,0:T(8,128)}, u32[]{:S(2)}) copy-start(s32[32,128,128]{2,1,0:T(8,128)} %param.20) | copy-start | bytes 6291460
  239.5 7.3 copy-start.10
  239.5 7.3 copy-start.11
  328.4 64.5 %all-to-all-start = ((f32[4,1,327680]{2,1,0:T(1,128)}), f32[4,1,327680]{2,1,0:T(1,128)}, u32[]{:S(2)}, u32[]{:S(2)}) async-start(f32[4,1,327680]{2,1,0:T(1,128)} %reshape.667), calls=%async_computation | async-start | bytes 10485760 | tf_op jit(solution)/shard_map/all_to_all | solution.py:106
  470.4 8.8 copy-start.8
  483.6 3.1 copy-start.13
  911.9 7.2 copy-start.9
  968.5 64.5 %all-to-all-start.1 = ((f32[4,1,327680]{2,1,0:T(1,128)}), f32[4,1,327680]{2,1,0:T(1,128)}, u32[]{:S(2)}, u32[]{:S(2)}) async-start(f32[4,1,327680]{2,1,0:T(1,128)} %reshape.669), calls=%async_computation.1 | async-start | bytes 10485760 | tf_op jit(solution)/shard_map/all_to_all | solution.py:152
  973.5 432.0 %all-reduce.5.cloned.1.call-start = ((), (), s32[]{:S(2)}) async-start(), calls=%async_computation.3 | async-start | bytes 4194304 | tf_op jit(solution)/shard_map/psum | solution.py:188
  1138.8 69.9 %copy-start.1 = (s32[32,128,128]{2,1,0:T(8,128)S(1)}, s32[32,128,128]{2,1,0:T(8,128)}, u32[]{:S(2)}) copy-start(s32[32,128,128]{2,1,0:T(8,128)} %param.20) | copy-start | bytes 6291460
  1138.8 69.9 %copy-start.2 = (s32[32,128,128]{2,1,0:T(8,128)S(1)}, s32[32,128,128]{2,1,0:T(8,128)}, u32[]{:S(2)}) copy-start(s32[32,128,128]{2,1,0:T(8,128)} %get-tuple-element.308) | copy-start | bytes 6291460
  1138.8 69.9 %copy-start.3 = (s32[32,128,128]{2,1,0:T(8,128)S(1)}, s32[32,128,128]{2,1,0:T(8,128)}, u32[]{:S(2)}) copy-start(s32[32,128,128]{2,1,0:T(8,128)} %get-tuple-element.309) | copy-start | bytes 6291460
  1138.8 69.9 %copy-start.4 = (s32[32,128,128]{2,1,0:T(8,128)S(1)}, s32[32,128,128]{2,1,0:T(8,128)}, u32[]{:S(2)}) copy-start(s32[32,128,128]{2,1,0:T(8,128)} %get-tuple-element.310) | copy-start | bytes 6291460
  1138.8 69.9 %copy-start.5 = (f32[32,128,128]{2,1,0:T(8,128)S(1)}, f32[32,128,128]{2,1,0:T(8,128)}, u32[]{:S(2)}) copy-start(f32[32,128,128]{2,1,0:T(8,128)} %get-tuple-element.290) | copy-start | bytes 6291460
  1138.8 69.9 %copy-start.6 = (f32[32,128,128]{2,1,0:T(8,128)S(1)}, f32[32,128,128]{2,1,0:T(8,128)}, u32[]{:S(2)}) copy-start(f32[32,128,128]{2,1,0:T(8,128)} %get-tuple-element.291) | copy-start | bytes 6291460
  1138.8 69.9 %copy-start.7 = (f32[32,128,128]{2,1,0:T(8,128)S(1)}, f32[32,128,128]{2,1,0:T(8,128)}, u32[]{:S(2)}) copy-start(f32[32,128,128]{2,1,0:T(8,128)} %get-tuple-element.292) | copy-start | bytes 6291460
  1138.8 69.9 %copy-start.15 = (f32[128]{0:T(128)S(1)}, f32[128]{0:T(128)}, u32[]{:S(2)}) copy-start(f32[128]{0:T(128)} %copy-done.14) | copy-start | bytes 1540
Sparse Core Ops, SparseCore 0:
  11.0 105.0 all-reduce.2
  1304.8 100.6 all-reduce.4
where the time goes:
time: 1430 us; the launch traced here: 1420 us
  matrix products  482 us (34%)
  local copies, waits for them, and re-layouts  368 us (26%)
  waiting for transfers between devices  313 us (22%)
  loops' own time  128 us (9%)
  other arithmetic  99.7 us (7%)
    dot_general x76, matrix products, contract(): return jnp.einsum(pattern, operand, matrix, precision=lax.Precision.HIGHEST)  482 us
    another operation x1, loops' own time, per_device(): mixed = lax.map(mix_row, jnp.arange(grid_part, dtype=jnp.int32))  128 us
    psum x1, waiting for transfers between devices, per_device(): return lax.psum(partial_potential, 'band')  101 us
    psum x1, waiting for transfers between devices, per_device(): density = lax.psum(partial_density[0], 'band')  98.9 us
    unnamed x39, local copies, waits for them, and re-layouts  92 us
    all_to_all x1, waiting for transfers between devices, per_device(): lax.all_to_all(jnp.stack([ywave_real, ywave_imag]), 'grid', split_axis=4,...  59.3 us
    all_to_all x1, waiting for transfers between devices, per_device(): lax.all_to_all(jnp.stack([inverse_real, inverse_imag], axis=1), 'grid', s...  53 us
    all_to_all x3, local copies, waits for them, and re-layouts, per_device(): lax.all_to_all(jnp.stack([ywave_real, ywave_imag]), 'grid', split_axis=4,...  42.8 us
  transfers between devices with their start and end apart: 4, of which 4 were waited for; matrix products, arithmetic and copies ran while one was open for 1% of the time, Pallas kernels for 0%

commit v1 on v0

--- a/solution.py
+++ b/solution.py
@@ -76,7 +76,9 @@
     first_band = band_at == 0
     lower_rows = (full_range >= 1) & (full_range < half)
     upper_rows = full_range > half
-    density = lax.psum(partial_density[0], "band")
+    density = partial_density[0]
+    for hop in (1, 2, 4):
+        density = density + lax.ppermute(density, "band", [(dev, dev ^ hop) for dev in range(8)])
     theta_fields = density[None] * node_fields(count_nodes, node_index, node_weight)
     cosine_z, sine_z = forward_tables(full_range, own_planes, length)
     forward_real = contract("axyz,zk->axyk", theta_fields, cosine_z)

time: 1430 us -> 1500 us (1.049)
  waiting for transfers between devices: 313 us -> 385 us
    ppermute x0 -> x3, waiting for transfers between devices: none -> 170 us  [per_device(): lax.ppermute(density, 'band', [(dev, dev ^ hop) for dev in range(8)])]
    psum x1 -> x0, waiting for transfers between devices: 98.9 us -> none  [per_device(): density = lax.psum(partial_density[0], 'band')]
    unnamed x39 -> x37, local copies, waits for them, and re-layouts: 92 us -> 91 us
  transfers between devices with their start and end apart: 4 -> 6, of which waited for: 4 -> 6; matrix products, arithmetic and copies ran while one was open for 1% -> 1% of each run, Pallas kernels for 0% -> 0%
where the time goes in v1:
time: 1500 us; the launch traced here: 1490 us
  matrix products  474 us (32%)
  waiting for transfers between devices  385 us (26%)
  local copies, waits for them, and re-layouts  370 us (25%)
  loops' own time  128 us (9%)
  other arithmetic  105 us (7%)
  starting transfers between devices  17.6 us (1%)
    dot_general x76, matrix products, contract(): return jnp.einsum(pattern, operand, matrix, precision=lax.Precision.HIGHEST)  474 us
    ppermute x3, waiting for transfers between devices, per_device(): lax.ppermute(density, 'band', [(dev, dev ^ hop) for dev in range(8)])  170 us
    another operation x1, loops' own time, per_device(): mixed = lax.map(mix_row, jnp.arange(grid_part, dtype=jnp.int32))  128 us
    psum x1, waiting for transfers between devices, per_device(): return lax.psum(partial_potential, 'band')  102 us
    unnamed x37, local copies, waits for them, and re-layouts  91 us
    all_to_all x1, waiting for transfers between devices, per_device(): lax.all_to_all(jnp.stack([ywave_real, ywave_imag]), 'grid', split_axis=4,...  59.3 us
    all_to_all x1, waiting for transfers between devices, per_device(): lax.all_to_all(jnp.stack([inverse_real, inverse_imag], axis=1), 'grid', s...  53 us
    all_to_all x3, local copies, waits for them, and re-layouts, per_device(): lax.all_to_all(jnp.stack([ywave_real, ywave_imag]), 'grid', split_axis=4,...  42.8 us
  transfers between devices with their start and end apart: 6, of which 6 were waited for; matrix products, arithmetic and copies ran while one was open for 1% of the time, Pallas kernels for 0%

profile of v1, /device:TPU:0, one launch (start us, length us, event | category | flops | bytes accessed | tf_op | source)
XLA Modules:
  0.0 1493.7 jit_solution(5604005393075104709)
XLA Ops:
  9.5 45.8 %collective-permute-done = f32[32,128,128]{2,1,0:T(8,128)S(1)} collective-permute-done((f32[32,128,128]{2,1,0:T(8,128)}, f32[32,128,128]{2,1,0:T(8,128)S(1)}, u32[]{:S(2)}, u32[]{:S(2)}) %collective-permute-start) | collective-permute-done | bytes 2097184 | tf_op jit(solution)/shard_map/ppermute | solution.py:81
  59.1 45.0 %collective-permute-done.1 = f32[32,128,128]{2,1,0:T(8,128)S(1)} collective-permute-done((f32[32,128,128]{2,1,0:T(8,128)S(1)}, f32[32,128,128]{2,1,0:T(8,128)S(1)}, u32[]{:S(2)}, u32[]{:S(2)}) %collective-permute-start.1) | collective-permute-done | bytes 2097184 | tf_op jit(solution)/shard_map/ppermute | solution.py:81
  118.3 79.5 %collective-permute-done.2 = f32[32,128,128]{2,1,0:T(8,128)} collective-permute-done((f32[32,128,128]{2,1,0:T(8,128)}, f32[32,128,128]{2,1,0:T(8,128)}, u32[]{:S(2)}, u32[]{:S(2)}) %collective-permute-start.2) | collective-permute-done | bytes 2097184 | tf_op jit(solution)/shard_map/ppermute | solution.py:81
  201.7 57.8 %fusion.70 = f32[1,20,32,128,8]{3,4,2,1,0:T(8,128)} fusion(f32[32,128,128]{2,1,0:T(8,128)} %get-tuple-element.295, s32[32,128,128]{2,1,0:T(8,128)} %get-tuple-element.309, f32[32,128,128]{2,1,0:T(8,128)} %get-tuple-element.296, s32[32,128,128]{2,1,0:T(8,128)} %get-tuple-element.310, f32[32,128,128]{2,1,0:T(8,128)} %get-tuple-element.294, ...), kind=kOutput, calls=%fused_computation.132 | convolution fusion | flops 1132476416 | bytes 21495840 | tf_op jit(solution)/shard_map/axyz,zk->axyk/dot_general | solution.py:39
  259.5 57.5 %negate_bitcast_fusion = f32[1,20,32,128,8]{3,4,2,1,0:T(8,128)} fusion(f32[32,128,128]{2,1,0:T(8,128)} %get-tuple-element.295, s32[32,128,128]{2,1,0:T(8,128)} %get-tuple-element.309, f32[32,128,128]{2,1,0:T(8,128)} %get-tuple-element.296, s32[32,128,128]{2,1,0:T(8,128)} %get-tuple-element.310, f32[32,128,128]{2,1,0:T(8,128)} %get-tuple-element.294, ...), kind=kOutput, calls=%fused_computation.123 | convolution fusion | flops 1133132800 | bytes 21496360 | tf_op jit(solution)/shard_map/axyz,zk->axyk/dot_general | solution.py:39
  351.0 9.3 scatter.14
  364.8 17.6 %copy.61 = f32[2,20,32,8,128]{2,3,1,0,4:T(8,128)} copy(f32[2,20,32,8,128]{4,3,2,1,0:T(8,128)} %pad_maximum_fusion.1) | data formatting | bytes 10485760 | tf_op jit(solution)/shard_map/stack | solution.py:109
  382.5 23.5 %reshape.667 = f32[4,1,327680]{2,1,0:T(1,128)} reshape(f32[128,2,20,8,32]{4,3,2,1,0:T(8,128)} %bitcast.307) | data formatting | bytes 10485760
  411.2 59.3 %all-to-all-done = f32[4,1,327680]{2,1,0:T(1,128)} async-done(((f32[4,1,327680]{2,1,0:T(1,128)}), f32[4,1,327680]{2,1,0:T(1,128)}, u32[]{:S(2)}, u32[]{:S(2)}) %all-to-all-start) | async-done | bytes 5242912 | tf_op jit(solution)/shard_map/all_to_all | solution.py:108
  471.0 17.8 %reduce.21 = f32[4,327680]{1,0:T(4,128)} reduce(f32[4,1,327680]{2,1,0:T(1,128)} %all-to-all-done, f32[]{:T(128)} %broadcast.766), dimensions={1}, to_apply=%all_to_all.26.reduce_sub_computation | reduce | bytes 10485764 | tf_op jit(solution)/shard_map/all_to_all | solution.py:108
  488.9 16.7 %reshape.668 = f32[128,2,20,8,32]{4,3,2,1,0:T(8,128)} reshape(f32[4,327680]{1,0:T(4,128)} %reduce.21) | data formatting | bytes 10485760
  505.6 25.8 %copy.142 = f32[2,20,32,8,4,32]{2,4,5,3,1,0:T(4,128)} copy(f32[2,20,32,8,4,32]{2,3,1,0,5,4:T(8,128)} %bitcast.308) | data formatting | bytes 10485760 | tf_op jit(solution)/shard_map/all_to_all | solution.py:108
  531.4 16.5 %all_to_all.29 = f32[2,20,128,8,32]{2,4,3,1,0:T(8,128)} reshape(f32[2,20,4,32,8,32]{3,2,5,4,1,0:T(4,128)} %bitcast.309) | data formatting | bytes 10485760 | tf_op jit(solution)/shard_map/all_to_all | solution.py:108
  564.2 424.3 %while.20 = (s32[]{:T(128)}, f32[32,2,20,8,128]{4,3,2,1,0:T(8,128)}, s32[32]{0:T(128)S(1)}, f32[20,8,32,128]{3,2,1,0:T(8,128)}, s32[8,32]{0,1:T(8,128)S(1)}, /*i...) while((s32[]{:T(128)}, ...), condition=%wide.region_1.2_spmd.clone.clone, body=%wide.region_0.1_spmd.clone.clone.sunk | while | flops 633025536 | bytes 4581378 | solution.py:149
  1004.0 17.6 %copy.63 = f32[32,2,20,8,128]{0,3,2,1,4:T(8,128)} copy(f32[32,2,20,8,128]{4,3,2,1,0:T(8,128)} %pad_maximum_fusion.2) | data formatting | bytes 10485760 | tf_op jit(solution)/shard_map/stack | solution.py:155
  1021.6 23.5 %reshape.669 = f32[4,1,327680]{2,1,0:T(1,128)} reshape(f32[128,2,20,8,32]{4,3,2,1,0:T(8,128)} %bitcast.310) | data formatting | bytes 10485760
  1056.6 53.0 %all-to-all-done.1 = f32[4,1,327680]{2,1,0:T(1,128)} async-done(((f32[4,1,327680]{2,1,0:T(1,128)}), f32[4,1,327680]{2,1,0:T(1,128)}, u32[]{:S(2)}, u32[]{:S(2)}) %all-to-all-start.1) | async-done | bytes 5242912 | tf_op jit(solution)/shard_map/all_to_all | solution.py:154
  1109.6 18.2 %reduce.22 = f32[4,327680]{1,0:T(4,128)} reduce(f32[4,1,327680]{2,1,0:T(1,128)} %all-to-all-done.1, f32[]{:T(128)} %broadcast.766), dimensions={1}, to_apply=%all_to_all.30.reduce_sub_computation | reduce | bytes 10485764 | tf_op jit(solution)/shard_map/all_to_all | solution.py:154
  1127.8 16.7 %reshape.670 = f32[128,2,20,8,32]{4,3,2,1,0:T(8,128)} reshape(f32[4,327680]{1,0:T(4,128)} %reduce.22) | data formatting | bytes 10485760
  1144.5 25.5 %copy.64 = f32[4,32,2,20,8,32]{1,0,5,3,4,2:T(4,128)} copy(f32[4,32,2,20,8,32]{1,4,3,2,5,0:T(8,128)} %bitcast.311) | data formatting | bytes 10485760 | tf_op jit(solution)/shard_map/all_to_all | solution.py:154
  1170.1 16.7 %all_to_all.33 = f32[128,2,20,8,32]{0,4,2,3,1:T(8,128)} reshape(f32[4,32,2,20,8,32]{1,0,5,3,4,2:T(4,128)} %copy.64) | data formatting | bytes 10485760 | tf_op jit(solution)/shard_map/all_to_all | solution.py:154
  1215.4 69.8 %fusion.68 = f32[20,32,128,128]{3,2,1,0:T(8,128)} fusion(f32[20,8,32,128]{3,2,1,0:T(8,128)S(1)} %get-tuple-element.284, s32[8]{0:T(128)S(1)} %iota_add_fusion.1, pred[8]{0:T(512)(128)(4,1)S(1)} %broadcast_compare_fusion), kind=kOutput, calls=%fused_computation.121 | convolution fusion | flops 1006649344 | bytes 44564520 | tf_op jit(solution)/shard_map/bpxy,pz->bxyz/dot_general | solution.py:39
  1285.3 95.9 %multiply_reduce_fusion.4 = f32[32,128,128]{2,1,0:T(8,128)} fusion(f32[20,32,128,128]{3,2,1,0:T(8,128)} %fusion.68, f32[32,128,128]{2,1,0:T(8,128)S(1)} %copy-done.6, f32[32,128,128]{2,1,0:T(8,128)S(1)} %copy-done.7, f32[32,128,128]{2,1,0:T(8,128)S(1)} %copy-done.5, f32[32,128,128]{2,1,0:T(8,128)S(1)} %get-tuple-element.289, ...), kind=kOutput, calls=%fused_computation.74 | convolution fusion | flops 1163411456 | bytes 63439400 | tf_op jit(solution)/shard_map/bpxy,pz->bxyz/dot_general | solution.py:39
  1381.2 102.3 %all-reduce.2.cloned.1.call-done = f32[32,128,128]{2,1,0:T(8,128)} async-done(((f32[32,128,128]{2,1,0:T(8,128)}), f32[32,128,128]{2,1,0:T(8,128)}) %all-reduce.2.cloned.1.call-update) | async-done | bytes 2097168 | tf_op jit(solution)/shard_map/psum | solution.py:190
  (1145 shorter events, 440.2 us)
Async XLA Ops:
  6.5 101.8 %copy-start = (s32[32,128,128]{2,1,0:T(8,128)S(1)}, s32[32,128,128]{2,1,0:T(8,128)}, u32[]{:S(2)}) copy-start(s32[32,128,128]{2,1,0:T(8,128)} %param.20) | copy-start | bytes 6291460
  6.5 48.8 %collective-permute-start = (f32[32,128,128]{2,1,0:T(8,128)}, f32[32,128,128]{2,1,0:T(8,128)S(1)}, u32[]{:S(2)}, u32[]{:S(2)}) collective-permute-start(f32[32,128,128]{2,1,0:T(8,128)} %bitcast.330), channel_id=1, source_target_pairs={{0,4},{4,0},{8,12},{12,8},{16,20},{20,16},{24,28},{28,24},{1,5},{5... | collective-permute-start | bytes 6291464 | tf_op jit(solution)/shard_map/ppermute | solution.py:81
  57.2 46.9 %collective-permute-start.1 = (f32[32,128,128]{2,1,0:T(8,128)S(1)}, f32[32,128,128]{2,1,0:T(8,128)S(1)}, u32[]{:S(2)}, u32[]{:S(2)}) collective-permute-start(f32[32,128,128]{2,1,0:T(8,128)S(1)} %bitcast_add_fusion.1), channel_id=1, source_target_pairs={{0,8},{4,12},{8,0},{12,4},{16,24},{20,28},{24,16},{28,20},{1,9},{5... | collective-permute-start | bytes 6291464 | tf_op jit(solution)/shard_map/ppermute | solution.py:81
  105.7 92.1 %collective-permute-start.2 = (f32[32,128,128]{2,1,0:T(8,128)}, f32[32,128,128]{2,1,0:T(8,128)}, u32[]{:S(2)}, u32[]{:S(2)}) collective-permute-start(f32[32,128,128]{2,1,0:T(8,128)} %add.498), channel_id=1, source_target_pairs={{0,16},{4,20},{8,24},{12,28},{16,0},{20,4},{24,8},{28,12},{1,17},{... | collective-permute-start | bytes 6291464 | tf_op jit(solution)/shard_map/ppermute | solution.py:81
  108.3 151.3 %copy-start.13 = (f32[128]{0:T(128)}, f32[128]{0:T(128)S(1)}, u32[]{:S(2)}) copy-start(f32[128]{0:T(128)S(1)} %fusion.141) | copy-start | bytes 1540
  317.1 7.3 copy-start.10
  317.1 7.3 copy-start.11
  406.0 64.5 %all-to-all-start = ((f32[4,1,327680]{2,1,0:T(1,128)}), f32[4,1,327680]{2,1,0:T(1,128)}, u32[]{:S(2)}, u32[]{:S(2)}) async-start(f32[4,1,327680]{2,1,0:T(1,128)} %reshape.667), calls=%async_computation | async-start | bytes 10485760 | tf_op jit(solution)/shard_map/all_to_all | solution.py:108
  547.9 8.8 copy-start.8
  561.1 3.1 copy-start.12
  988.5 7.3 copy-start.9
  1045.1 64.5 %all-to-all-start.1 = ((f32[4,1,327680]{2,1,0:T(1,128)}), f32[4,1,327680]{2,1,0:T(1,128)}, u32[]{:S(2)}, u32[]{:S(2)}) async-start(f32[4,1,327680]{2,1,0:T(1,128)} %reshape.669), calls=%async_computation.1 | async-start | bytes 10485760 | tf_op jit(solution)/shard_map/all_to_all | solution.py:154
  1050.1 433.4 %all-reduce.2.cloned.1.call-start = ((), (), s32[]{:S(2)}) async-start(), calls=%async_computation.2 | async-start | bytes 4194304 | tf_op jit(solution)/shard_map/psum | solution.py:190
  1215.3 69.9 %copy-start.1 = (s32[32,128,128]{2,1,0:T(8,128)S(1)}, s32[32,128,128]{2,1,0:T(8,128)}, u32[]{:S(2)}) copy-start(s32[32,128,128]{2,1,0:T(8,128)} %param.20) | copy-start | bytes 6291460
  1215.3 69.9 %copy-start.2 = (s32[32,128,128]{2,1,0:T(8,128)S(1)}, s32[32,128,128]{2,1,0:T(8,128)}, u32[]{:S(2)}) copy-start(s32[32,128,128]{2,1,0:T(8,128)} %get-tuple-element.308) | copy-start | bytes 6291460
  1215.4 69.9 %copy-start.3 = (s32[32,128,128]{2,1,0:T(8,128)S(1)}, s32[32,128,128]{2,1,0:T(8,128)}, u32[]{:S(2)}) copy-start(s32[32,128,128]{2,1,0:T(8,128)} %get-tuple-element.309) | copy-start | bytes 6291460
  1215.4 69.9 %copy-start.4 = (s32[32,128,128]{2,1,0:T(8,128)S(1)}, s32[32,128,128]{2,1,0:T(8,128)}, u32[]{:S(2)}) copy-start(s32[32,128,128]{2,1,0:T(8,128)} %get-tuple-element.310) | copy-start | bytes 6291460
  1215.4 69.9 %copy-start.5 = (f32[32,128,128]{2,1,0:T(8,128)S(1)}, f32[32,128,128]{2,1,0:T(8,128)}, u32[]{:S(2)}) copy-start(f32[32,128,128]{2,1,0:T(8,128)} %get-tuple-element.290) | copy-start | bytes 6291460
  1215.4 69.9 %copy-start.6 = (f32[32,128,128]{2,1,0:T(8,128)S(1)}, f32[32,128,128]{2,1,0:T(8,128)}, u32[]{:S(2)}) copy-start(f32[32,128,128]{2,1,0:T(8,128)} %get-tuple-element.291) | copy-start | bytes 6291460
  1215.4 69.9 %copy-start.7 = (f32[32,128,128]{2,1,0:T(8,128)S(1)}, f32[32,128,128]{2,1,0:T(8,128)}, u32[]{:S(2)}) copy-start(f32[32,128,128]{2,1,0:T(8,128)} %get-tuple-element.292) | copy-start | bytes 6291460
  1215.4 69.9 %copy-start.14 = (f32[128]{0:T(128)S(1)}, f32[128]{0:T(128)}, u32[]{:S(2)}) copy-start(f32[128]{0:T(128)} %copy-done.13) | copy-start | bytes 1540
Sparse Core Ops, SparseCore 0:
  1381.4 102.1 all-reduce.1
